TPU v7x, 8 devices: a whole 2x2x1 slice. The times are simulated.
8 devices in a mesh: dp: 1 (over z), tp: 8 (over y, x, core).
Axes of the slice: x: 2, y: 2, z: 1, core: 2. Of those that a mesh axis runs over, the one named last changes fastest.
Arguments:
- tokens: int32 [48], P('dp')
- positions: int32 [48], P('dp')
- self_keys: bfloat16 [2, 48, 448, 8, 64], P(None, 'dp', None, 'tp')
- self_vals: bfloat16 [2, 48, 448, 8, 64], P(None, 'dp', None, 'tp')
- cross_keys: bfloat16 [2, 48, 1500, 8, 64], P(None, 'dp', None, 'tp')
- cross_vals: bfloat16 [2, 48, 1500, 8, 64], P(None, 'dp', None, 'tp')
- embed_table: bfloat16 [52224, 512], P('tp')
- pos_table: bfloat16 [448, 512], replicated
- w_qkv: bfloat16 [2, 512, 3, 8, 64], P(None, None, None, 'tp')
- w_cq: bfloat16 [2, 512, 8, 64], P(None, None, 'tp')
- in_bias: float32 [2, 3, 8, 64], P(None, None, 'tp')
- w_out: bfloat16 [2, 2, 8, 64, 512], P(None, None, 'tp')
- out_bias: float32 [2, 3, 512], replicated
- w_fc1: bfloat16 [2, 512, 2048], P(None, None, 'tp')
- b_fc1: float32 [2, 2048], P(None, 'tp')
- w_fc2: bfloat16 [2, 2048, 512], P(None, 'tp')
- ln_layers: float32 [2, 3, 2, 512], replicated
- ln_final: float32 [2, 512], replicated
Outputs:
- output 1: float32 [48, 52224], P('dp', 'tp')
- output 2: bfloat16 [2, 48, 448, 8, 64], P(None, 'dp', None, 'tp')
- output 3: bfloat16 [2, 48, 448, 8, 64], P(None, 'dp', None, 'tp')
All inputs are finite; a program needn't handle non-finite values.
Results may differ from a plain program's by a relative error of at most 0.012397.
Values are sent between devices in bfloat16 or wider.
A program may use at most 1 GiB of HBM per device.

v0:
```python
import jax
import jax.numpy as jnp
from jax import lax
from jax.sharding import PartitionSpec as P


def layer_norm(residual, ln_gain, ln_shift):
    row_mean = jnp.mean(residual, axis=-1, keepdims=True)
    centred = residual - row_mean
    variance = jnp.mean(centred * centred, axis=-1, keepdims=True)
    return (centred * lax.rsqrt(variance + 1e-5) * ln_gain + ln_shift).astype(jnp.bfloat16)


def cross_attend(queries, key_rows, val_rows):
    scores = jnp.einsum('bhe,bthe->bht', queries, key_rows, preferred_element_type=jnp.float32) * (queries.shape[-1] ** -0.5)
    weights = jax.nn.softmax(scores, axis=-1).astype(jnp.bfloat16)
    return jnp.einsum('bht,bthe->bhe', weights, val_rows, preferred_element_type=jnp.float32).astype(jnp.bfloat16)


def self_attend(queries, key_new, val_new, cache_keys, cache_vals, mask_add):
    qk_scale = queries.shape[-1] ** -0.5
    past_scores = jnp.einsum('bhe,bthe->bht', queries, cache_keys, preferred_element_type=jnp.float32) * qk_scale + mask_add
    new_score = jnp.einsum('bhe,bhe->bh', queries, key_new, preferred_element_type=jnp.float32)[:, :, None] * qk_scale
    score_peak = jnp.maximum(jnp.max(past_scores, axis=-1, keepdims=True), new_score)
    past_exp = jnp.exp(past_scores - score_peak)
    new_exp = jnp.exp(new_score - score_peak)
    denominator = jnp.sum(past_exp, axis=-1, keepdims=True) + new_exp
    past_weight = (past_exp / denominator).astype(jnp.bfloat16)
    new_weight = (new_exp / denominator).astype(jnp.bfloat16)
    mixed_vals = jnp.einsum('bht,bthe->bhe', past_weight, cache_vals, preferred_element_type=jnp.float32)
    mixed_vals = mixed_vals + new_weight.astype(jnp.float32) * val_new.astype(jnp.float32)
    return mixed_vals.astype(jnp.bfloat16)


def group_sum(part_sum):
    return lax.psum(part_sum, 'tp').astype(jnp.bfloat16).astype(jnp.float32)


def solution(mesh):
    def local_step(tokens, positions, self_keys, self_vals, cross_keys, cross_vals, embed_table, pos_table, w_qkv, w_cq, in_bias, w_out, out_bias, w_fc1, b_fc1, w_fc2, ln_layers, ln_final):
        shard_rows = embed_table.shape[0]
        local_ids = tokens - lax.axis_index('tp') * shard_rows
        owned_mask = (local_ids >= 0) & (local_ids < shard_rows)
        picked = jnp.take(embed_table, jnp.clip(local_ids, 0, shard_rows - 1), axis=0)
        picked = jnp.where(owned_mask[:, None], picked, jnp.zeros_like(picked))
        residual = lax.psum(picked, 'tp').astype(jnp.float32) + jnp.take(pos_table, positions, axis=0).astype(jnp.float32)
        cache_pos = jnp.arange(self_keys.shape[2])[None, :]
        mask_add = jnp.where(cache_pos < positions[:, None], 0.0, -1e30)[:, None, :]
        new_key_rows = []
        new_val_rows = []
        for layer_idx in range(self_keys.shape[0]):
            ln_params = ln_layers[layer_idx]
            bias_in = in_bias[layer_idx]
            hidden = layer_norm(residual, ln_params[0, 0], ln_params[0, 1])
            projected = jnp.einsum('bd,dthe->bthe', hidden, w_qkv[layer_idx], preferred_element_type=jnp.float32)
            queries = (projected[:, 0] + bias_in[0]).astype(jnp.bfloat16)
            key_new = projected[:, 1].astype(jnp.bfloat16)
            val_new = (projected[:, 2] + bias_in[1]).astype(jnp.bfloat16)
            attended = self_attend(queries, key_new, val_new, self_keys[layer_idx], self_vals[layer_idx], mask_add)
            head_sum = jnp.einsum('bhe,hed->bd', attended, w_out[layer_idx, 0], preferred_element_type=jnp.float32)
            residual = residual + group_sum(head_sum) + out_bias[layer_idx, 0]
            hidden = layer_norm(residual, ln_params[1, 0], ln_params[1, 1])
            cross_q = (jnp.einsum('bd,dhe->bhe', hidden, w_cq[layer_idx], preferred_element_type=jnp.float32) + bias_in[2]).astype(jnp.bfloat16)
            attended = cross_attend(cross_q, cross_keys[layer_idx], cross_vals[layer_idx])
            head_sum = jnp.einsum('bhe,hed->bd', attended, w_out[layer_idx, 1], preferred_element_type=jnp.float32)
            residual = residual + group_sum(head_sum) + out_bias[layer_idx, 1]
            hidden = layer_norm(residual, ln_params[2, 0], ln_params[2, 1])
            fc1_out = jnp.dot(hidden, w_fc1[layer_idx], preferred_element_type=jnp.float32) + b_fc1[layer_idx]
            active = jax.nn.gelu(fc1_out, approximate=False).astype(jnp.bfloat16)
            fc2_out = jnp.dot(active, w_fc2[layer_idx], preferred_element_type=jnp.float32)
            residual = residual + group_sum(fc2_out) + out_bias[layer_idx, 2]
            new_key_rows.append(key_new)
            new_val_rows.append(val_new)
        final_hidden = layer_norm(residual, ln_final[0], ln_final[1])
        logits = jnp.einsum('bd,vd->bv', final_hidden, embed_table, preferred_element_type=jnp.float32)
        write_mask = (cache_pos == positions[:, None])[None, :, :, None, None]
        new_keys = jnp.where(write_mask, jnp.stack(new_key_rows)[:, :, None], self_keys)
        new_vals = jnp.where(write_mask, jnp.stack(new_val_rows)[:, :, None], self_vals)
        return logits, new_keys, new_vals

    batch_spec = P('dp')
    cache_spec = P(None, 'dp', None, 'tp', None)
    in_specs = (batch_spec, batch_spec, cache_spec, cache_spec, cache_spec, cache_spec, P('tp', None), P(None, None), P(None, None, None, 'tp', None), P(None, None, 'tp', None), P(None, None, 'tp', None), P(None, None, 'tp', None, None), P(None, None, None), P(None, None, 'tp'), P(None, 'tp'), P(None, 'tp', None), P(None, None, None, None), P(None, None))
    out_specs = (P('dp', 'tp'), cache_spec, cache_spec)
    return jax.shard_map(local_step, mesh=mesh, in_specs=in_specs, out_specs=out_specs, check_vma=False)
```

profile of v0, /device:TPU:0, one launch (start us, length us, event | category | flops | bytes accessed | tf_op | source)
XLA Modules:
  0.0 241.7 jit_solution(15138505333629587340)
XLA Ops:
  0.7 0.7 compare_and_fusion
  1.4 0.7 compare_select_fusion
  2.1 0.7 compare_and_fusion.1
  2.7 0.8 fusion.293
  3.5 0.7 slice_bitcast_fusion.8
  4.3 0.8 fusion.292
  5.0 0.8 fusion.291
  5.8 0.7 iota_compare_fusion
  6.6 0.7 slice_bitcast_fusion.6
  7.3 0.7 gather_fusion.1
  8.0 4.4 %gather_fusion = bf16[48,512]{1,0:T(8,128)(2,1)S(1)} fusion(bf16[6528,512]{1,0:T(8,128)(2,1)} %param.24, s32[1024]{0:T(1024)S(1)} %pad_clamp_fusion.1), kind=kCustom, calls=%fused_computation | custom fusion | bytes 98496 | tf_op jit(solution)/shard_map/jit(_take)/gather | solution.py:44
  12.5 25.5 %psum.49 = bf16[48,512]{1,0:T(8,128)(2,1)S(1)} all-reduce(bf16[48,512]{1,0:T(8,128)(2,1)S(1)} %select_select_fusion), channel_id=1, replica_groups=mesh['dp'=1,'tp'=8] {'tp'}, use_global_device_ids=true, to_apply=%region_0.1 | all-reduce | flops 24576 | bytes 98304 | tf_op jit(solution)/shard_map/psum | solution.py:46
  38.4 1.2 fusion.44
  39.7 2.4 fusion.18
  42.2 0.9 fusion.281
  43.0 0.9 fusion.49
  43.9 0.8 fusion.119
  44.7 2.8 %fusion.16 = f32[48,1,64]{2,1,0:T(1,128)S(1)} fusion(bf16[2,48,448,1,64]{2,4,3,1,0:T(8,128)(2,1)} %param.21, bf16[48,448,1]{1,0,2:T(8,128)(2,1)S(1)} %fusion.119), kind=kOutput, calls=%fused_computation.20 | convolution fusion | flops 2752512 | bytes 3201024 | tf_op jit(solution)/shard_map/bht,bthe->bhe/dot_general | solution.py:30
  47.7 23.8 %psum.50 = bf16[48,512]{1,0:T(8,128)(2,1)S(1)} all-reduce(f32[48,512]{1,0:T(8,128)S(1)} %fusion.60), channel_id=1, replica_groups=mesh['dp'=1,'tp'=8] {'tp'}, use_global_device_ids=true, to_apply=%region_5.6 | all-reduce | flops 24576 | bytes 147456 | tf_op jit(solution)/shard_map/psum | solution.py:36
  72.1 5.0 %fusion.6 = f32[48,1,1500]{2,1,0:T(1,128)S(1)} fusion(bf16[2,48,1500,1,64]{2,4,3,1,0:T(8,128)(2,1)} %param.22, bf16[48,64,1]{1,0,2:T(8,128)(2,1)S(1)} %fusion.27), kind=kOutput, calls=%fused_computation.8 | convolution fusion | flops 9216000 | bytes 9731328 | tf_op jit(solution)/shard_map/bhe,bthe->bht/dot_general | solution.py:15
  77.7 6.2 %fusion.4 = f32[48,1,64]{2,1,0:T(1,128)S(1)} fusion(bf16[2,48,1500,1,64]{2,4,3,1,0:T(8,128)(2,1)} %param.23, bf16[48,1500,1]{1,0,2:T(8,128)(2,1)S(1)} %fusion.45), kind=kOutput, calls=%fused_computation.6 | convolution fusion | flops 9216000 | bytes 9593472 | tf_op jit(solution)/shard_map/bht,bthe->bhe/dot_general | solution.py:17
  84.0 24.8 %psum.51 = bf16[48,512]{1,0:T(8,128)(2,1)S(1)} all-reduce(f32[48,512]{1,0:T(8,128)S(1)} %fusion.57), channel_id=1, replica_groups=mesh['dp'=1,'tp'=8] {'tp'}, use_global_device_ids=true, to_apply=%region_10.11 | all-reduce | flops 24576 | bytes 147456 | tf_op jit(solution)/shard_map/psum | solution.py:36
  109.7 23.8 %psum.52 = bf16[48,512]{1,0:T(8,128)(2,1)S(1)} all-reduce(f32[48,512]{1,0:T(8,128)S(1)} %fusion.33), channel_id=1, replica_groups=mesh['dp'=1,'tp'=8] {'tp'}, use_global_device_ids=true, to_apply=%region_13.14 | all-reduce | flops 24576 | bytes 147456 | tf_op jit(solution)/shard_map/psum | solution.py:36
  134.2 2.4 fusion.14
  137.2 2.8 %fusion.12 = f32[48,1,64]{2,1,0:T(1,128)S(1)} fusion(bf16[2,48,448,1,64]{2,4,3,1,0:T(8,128)(2,1)} %param.21, bf16[48,448,1]{1,0,2:T(8,128)(2,1)S(1)} %fusion.120), kind=kOutput, calls=%fused_computation.16 | convolution fusion | flops 2752512 | bytes 3201024 | tf_op jit(solution)/shard_map/bht,bthe->bhe/dot_general | solution.py:30
  140.2 25.0 %psum.53 = bf16[48,512]{1,0:T(8,128)(2,1)S(1)} all-reduce(f32[48,512]{1,0:T(8,128)S(1)} %fusion.55), channel_id=1, replica_groups=mesh['dp'=1,'tp'=8] {'tp'}, use_global_device_ids=true, to_apply=%region_18.19 | all-reduce | flops 24576 | bytes 147456 | tf_op jit(solution)/shard_map/psum | solution.py:36
  165.7 5.0 %fusion.2 = f32[48,1,1500]{2,1,0:T(1,128)S(1)} fusion(bf16[2,48,1500,1,64]{2,4,3,1,0:T(8,128)(2,1)} %param.22, bf16[48,64,1]{1,0,2:T(8,128)(2,1)S(1)} %fusion.26), kind=kOutput, calls=%fused_computation.4 | convolution fusion | flops 9216000 | bytes 9731328 | tf_op jit(solution)/shard_map/bhe,bthe->bht/dot_general | solution.py:15
  171.2 6.2 %fusion = f32[48,1,64]{2,1,0:T(1,128)S(1)} fusion(bf16[2,48,1500,1,64]{2,4,3,1,0:T(8,128)(2,1)} %param.23, bf16[48,1500,1]{1,0,2:T(8,128)(2,1)S(1)} %fusion.46), kind=kOutput, calls=%fused_computation.2 | convolution fusion | flops 9216000 | bytes 9593472 | tf_op jit(solution)/shard_map/bht,bthe->bhe/dot_general | solution.py:17
  177.6 23.8 %psum.54 = bf16[48,512]{1,0:T(8,128)(2,1)S(1)} all-reduce(f32[48,512]{1,0:T(8,128)S(1)} %fusion.52), channel_id=1, replica_groups=mesh['dp'=1,'tp'=8] {'tp'}, use_global_device_ids=true, to_apply=%region_23.24 | all-reduce | flops 24576 | bytes 147456 | tf_op jit(solution)/shard_map/psum | solution.py:36
  202.2 24.8 %psum.55 = bf16[48,512]{1,0:T(8,128)(2,1)S(1)} all-reduce(f32[48,512]{1,0:T(8,128)S(1)} %fusion.30), channel_id=1, replica_groups=mesh['dp'=1,'tp'=8] {'tp'}, use_global_device_ids=true, to_apply=%region_26.27 | all-reduce | flops 24576 | bytes 147456 | tf_op jit(solution)/shard_map/psum | solution.py:36
  227.4 6.2 %fusion.78 = f32[48,6528]{1,0:T(8,128)} fusion(bf16[6528,512]{1,0:T(8,128)(2,1)} %param.24, f32[48,512]{1,0:T(8,128)S(1)} %get-tuple-element.4, f32[512]{0:T(512)S(1)} %bitcast.246, f32[512]{0:T(512)S(1)} %bitcast.245, f32[48]{0:T(128)S(1)} %add_rsqrt_fusion, f32[48]{0:T(128)S(1)} %broadcast_multiply_fusion), kind=kOutput, calls=%fused_computation.126 | convolution fusion | flops 320987136 | bytes 8040832 | tf_op jit(solution)/shard_map/bd,vd->bv/dot_general | solution.py:75
  233.6 8.1 %broadcast_select_fusion = (bf16[2,48,448,1,64]{2,4,3,1,0:T(8,128)(2,1)}, bf16[2,48,448,1,64]{2,4,3,1,0:T(8,128)(2,1)}) fusion(bf16[2,48,448,1,64]{2,4,3,1,0:T(8,128)(2,1)} %param.21, pred[48,448]{1,0:T(8,128)(4,1)S(1)} %iota_compare_fusion, bf16[2,48,64]{2,1,0:T(8,128)(2,1)S(1)} %maximum_bitcast_fusion.1, bf16[2,48,448,1,64]{2,4,3,1,0:T(8,128)(2,1)S(1)} %bitcast.239, ...), kind=kLoop, calls=%fused_computation.14 | loop fusion | flops 5505024 | bytes 22066176 | tf_op jit(solution)/shard_map/jit(_where)/select_n | solution.py:78
  (83 shorter events, 6.7 us)
Async XLA Ops:
  0.6 6.7 %copy-start = (bf16[448,512]{1,0:T(8,128)(2,1)S(1)}, bf16[448,512]{1,0:T(8,128)(2,1)}, u32[]{:S(2)}) copy-start(bf16[448,512]{1,0:T(8,128)(2,1)} %param.25) | copy-start | bytes 1376260
  0.6 46.8 %copy-start.2 = (bf16[2,2,1,64,512]{4,3,2,1,0:T(8,128)(2,1)S(1)}, bf16[2,2,1,64,512]{4,3,2,1,0:T(8,128)(2,1)}, u32[]{:S(2)}) copy-start(bf16[2,2,1,64,512]{4,3,2,1,0:T(8,128)(2,1)} %param.29) | copy-start | bytes 786436
  0.7 71.2 %copy-start.7 = (bf16[2,512,1,64]{1,3,2,0:T(8,128)(2,1)S(1)}, bf16[2,512,1,64]{1,3,2,0:T(8,128)(2,1)}, u32[]{:S(2)}) copy-start(bf16[2,512,1,64]{1,3,2,0:T(8,128)(2,1)} %param.27) | copy-start | bytes 393220
  77.2 31.9 %copy-start.4 = (bf16[2,256,512]{2,1,0:T(8,128)(2,1)S(1)}, bf16[2,256,512]{2,1,0:T(8,128)(2,1)}, u32[]{:S(2)}) copy-start(bf16[2,256,512]{2,1,0:T(8,128)(2,1)} %param.33) | copy-start | bytes 1572868
  77.3 31.9 %copy-start.5 = (bf16[2,512,256]{2,1,0:T(8,128)(2,1)S(1)}, bf16[2,512,256]{2,1,0:T(8,128)(2,1)}, u32[]{:S(2)}) copy-start(bf16[2,512,256]{2,1,0:T(8,128)(2,1)} %param.31) | copy-start | bytes 1572868
  77.6 56.2 %copy-start.6 = (bf16[2,512,3,1,64]{1,4,3,2,0:T(8,128)(2,1)S(1)}, bf16[2,512,3,1,64]{1,4,3,2,0:T(8,128)(2,1)}, u32[]{:S(2)}) copy-start(bf16[2,512,3,1,64]{1,4,3,2,0:T(8,128)(2,1)} %param.26) | copy-start | bytes 1179652
  77.6 59.0 %copy-start.3 = (s32[48]{0:T(128)S(1)}, s32[48]{0:T(128)}, u32[]{:S(2)}) copy-start(s32[48]{0:T(128)} %param.19) | copy-start | bytes 580
  202.2 31.4 %slice-start = ((s8[6291456]{0:T(1024)(128)(4,1)}), s8[2097152]{0:T(1024)(128)(4,1)S(1)}, s32[]{:S(2)}) async-start(s8[6291456]{0:T(1024)(128)(4,1)} %bitcast.238), calls=%async_computation | async-start | bytes 4194304
  227.4 6.2 %slice-start.1 = ((s8[6291456]{0:T(1024)(128)(4,1)}), s8[4194304]{0:T(1024)(128)(4,1)S(1)}, s32[]{:S(2)}) async-start(s8[6291456]{0:T(1024)(128)(4,1)} %bitcast.238), calls=%async_computation.1 | async-start | bytes 8388608
  233.6 8.1 %copy-start.1 = (bf16[448,512]{1,0:T(8,128)(2,1)S(1)}, bf16[448,512]{1,0:T(8,128)(2,1)}, u32[]{:S(2)}) copy-start(bf16[448,512]{1,0:T(8,128)(2,1)} %param.25) | copy-start | bytes 1376260
where the time goes:
time: 243 us; the launch traced here: 242 us
  blocking collectives  172 us (71%)
  matrix products  42.5 us (17%)
  other arithmetic  17.6 us (7%)
  local copies, waits for them, and re-layouts  8.97 us (4%)
    psum x6, blocking collectives, group_sum(): return lax.psum(part_sum, 'tp').astype(jnp.bfloat16).astype(jnp.float32)  146 us
    psum x1, blocking collectives, local_step(): lax.psum(picked, 'tp').astype(jnp.float32)  25.5 us
    dot_general x2, matrix products, cross_attend(): jnp.einsum('bht,bthe->bhe', weights, val_rows, preferred_element_type=jnp...  12.5 us
    dot_general x2, matrix products, cross_attend(): jnp.einsum('bhe,bthe->bht', queries, key_rows, preferred_element_type=jnp...  10 us
    select_n x1, other arithmetic, local_step(): jnp.where(write_mask, jnp.stack(new_val_rows)[:, :, None], self_vals)  8.08 us
    dot_general x1, matrix products, local_step(): jnp.einsum('bd,vd->bv', final_hidden, embed_table, preferred_element_type...  6.18 us
    dot_general x2, matrix products, self_attend(): jnp.einsum('bht,bthe->bhe', past_weight, cache_vals, preferred_element_ty...  5.59 us

commit v1 on v0

v1 whole, which is shorter than its diff:
```python
import functools

import jax
import jax.numpy as jnp
from jax import lax
from jax.experimental import pallas as pl
from jax.experimental.pallas import tpu as pltpu
from jax.sharding import PartitionSpec as P

MESH = pl.DeviceIdType.MESH
BF = jnp.bfloat16
F32 = jnp.float32
NT = (((1,), (1,)), ((), ()))
N_DEV = 8
CHIP_PEERS = (2, 4, 6)


def dot(a, b):
    return jnp.dot(a, b, preferred_element_type=F32)


def dot_nt(a, b):
    return lax.dot_general(a, b, NT, preferred_element_type=F32)


def layer_norm(x, gain, shift):
    mean = jnp.mean(x, axis=-1, keepdims=True)
    centred = x - mean
    var = jnp.mean(centred * centred, axis=-1, keepdims=True)
    return (centred * lax.rsqrt(var + 1e-5) * gain + shift).astype(BF)


def gelu(x):
    return 0.5 * x * (1.0 + lax.erf(x * (0.5 ** 0.5)))


def chain_kernel(tok, pos, sk, sv, ck, cv, emb, ptab, wqkv, wcq, inb, wout, outb, wf1, bf1, wf2, lns, lnf,
                 kc, vc, e_v, fin,
                 cross, pt_v, wqkv_v, wcq_v, inb_v, outb_v, wf1_v, bf1_v, wf2_v, lns_v, lnf_v, wo_full,
                 rs_src, rs_dst, ag_buf, o_buf,
                 load_sem, kv_sem, cross_sem, wo_sem,
                 rs_s, rs_r, ag_s, ag_r, o_s, o_r, w_s, w_r):
    me = lax.axis_index('tp')
    n_seq, depth = fin.shape
    n_layers = kc.shape[0]
    n_blk = n_seq // 8
    chunk = n_seq // 2
    shard_rows = e_v.shape[0] * 8

    def local(src, dst, sem):
        cp = pltpu.make_async_copy(src, dst, sem)
        cp.start()
        return cp

    def remote(src, dst, s_sem, r_sem, k):
        return pltpu.make_async_remote_copy(src_ref=src, dst_ref=dst, send_sem=s_sem, recv_sem=r_sem,
                                            device_id={'tp': me ^ k}, device_id_type=MESH)

    names = [(ptab, pt_v), (emb, e_v), (lns, lns_v), (lnf, lnf_v), (inb, inb_v), (outb, outb_v), (bf1, bf1_v), (wqkv, wqkv_v)]
    bulk = [local(s, d, load_sem.at[i]) for i, (s, d) in enumerate(names)]
    wo_own = [local(wout.at[s // 2, s % 2], wo_full.at[s, me], wo_sem.at[s]) for s in range(4)]
    k_load = [local(sk.at[0], kc.at[0], kv_sem.at[0, 0]), None]
    v_load = [local(sv.at[0], vc.at[0], kv_sem.at[1, 0]), None]
    late = [local(s, d, load_sem.at[8 + i]) for i, (s, d) in enumerate([(wcq, wcq_v), (wf1, wf1_v), (wf2, wf2_v)])]
    ck_load = [local(ck.at[0], cross.at[0], cross_sem.at[0]), None]
    cv_load = [local(cv.at[0], cross.at[1], cross_sem.at[1]), None]
    k_load[1] = local(sk.at[1], kc.at[1], kv_sem.at[0, 1])
    v_load[1] = local(sv.at[1], vc.at[1], kv_sem.at[1, 1])
    ck_load[1] = local(ck.at[1], cross.at[2], cross_sem.at[2])
    cross_slot = ((0, 1), (2, 0))

    bar = pltpu.get_barrier_semaphore()
    for k in range(1, N_DEV):
        pl.semaphore_signal(bar, inc=1, device_id={'tp': me ^ k}, device_id_type=MESH)
    pl.semaphore_wait(bar, N_DEV - 1)

    pick_row = lax.broadcasted_iota(jnp.int32, (8, 64), 0)
    pick_lane = lax.broadcasted_iota(jnp.int32, (8, 64), 1)

    def pick_rows(table, index_of, ok_of):
        blocks = []
        for m in range(n_blk):
            groups = []
            want = jnp.full((8, 64), -1, jnp.int32)
            for j in range(8):
                i = index_of(8 * m + j)
                groups.append(table[lax.div(i, 8)].astype(F32))
                at = 8 * j + lax.rem(i, 8)
                if ok_of is not None:
                    at = jnp.where(ok_of(8 * m + j), at, -1)
                want = jnp.where(pick_row == j, at, want)
            one_hot = jnp.where(pick_lane == want, 1.0, 0.0).astype(BF)
            blocks.append(dot(one_hot, jnp.concatenate(groups, axis=0).astype(BF)))
        return jnp.concatenate(blocks, axis=0)

    def rs_start(ph, part):
        for p in range(N_DEV):
            rs_src[ph, p] = part[chunk * (p % 2):chunk * (p % 2) + chunk, 128 * (p // 2):128 * (p // 2) + 128]
        cps = [remote(rs_src.at[ph, me ^ k], rs_dst.at[ph, k], rs_s.at[ph, k], rs_r.at[ph, k], k) for k in range(1, N_DEV)]
        for cp in cps:
            cp.start()
        return cps

    def rs_finish(ph, cps):
        total = rs_src[ph, me]
        for k, cp in zip(range(1, N_DEV), cps):
            cp.wait_recv()
            total = total + rs_dst[ph, k]
        return total

    def ag_start(ph, piece):
        ag_buf[ph, me] = piece
        cps = [remote(ag_buf.at[ph, me], ag_buf.at[ph, me], ag_s.at[ph, k], ag_r.at[ph, k], k) for k in range(1, N_DEV)]
        for cp in cps:
            cp.start()
        return cps

    def ag_finish(ph, cps):
        for cp in cps:
            cp.wait_recv()
        cols = [jnp.concatenate([ag_buf[ph, 2 * c].astype(F32), ag_buf[ph, 2 * c + 1].astype(F32)], axis=0) for c in range(4)]
        return jnp.concatenate(cols, axis=1)

    def o_start(ph, o):
        o_buf[ph, me] = o
        cps = [remote(o_buf.at[ph, me], o_buf.at[ph, me], o_s.at[ph, k], o_r.at[ph, k], k) for k in range(1, N_DEV)]
        for cp in cps:
            cp.start()
        return cps

    lane128 = lax.broadcasted_iota(jnp.int32, (n_seq, 128), 1)

    def o_finish(ph, cps):
        for cp in cps:
            cp.wait_recv()
        pieces = [jnp.where(lane128 < 64, o_buf[ph, 2 * c].astype(F32), o_buf[ph, 2 * c + 1].astype(F32)) for c in range(4)]
        return jnp.concatenate(pieces, axis=1).astype(BF)

    def w_direct(s):
        wo_own[s].wait()
        cps = {k: remote(wo_full.at[s, me], wo_full.at[s, me], w_s.at[s, k], w_r.at[s, k], k) for k in (2, 4, 6, 1)}
        for cp in cps.values():
            cp.start()
        return cps

    def w_relay(s, cps):
        out = {}
        for k in CHIP_PEERS:
            cps[k].wait_recv()
            out[k ^ 1] = remote(wo_full.at[s, me ^ k], wo_full.at[s, me ^ k], w_s.at[s, k ^ 1], w_r.at[s, k ^ 1], 1)
            out[k ^ 1].start()
        return out

    def w_finish(s, cps, rel):
        cps[1].wait_recv()
        for cp in rel.values():
            cp.wait_recv()

    bulk[0].wait()
    pos_rows = pick_rows(pt_v, lambda b: pos[b], None)
    bulk[1].wait()
    first = me * shard_rows

    def owned(b):
        loc = tok[b] - first
        return jnp.logical_and(loc >= 0, loc < shard_rows)

    part = pick_rows(e_v, lambda b: jnp.clip(tok[b] - first, 0, shard_rows - 1), owned)
    cps0 = rs_start(0, part)
    w_cps = [w_direct(0), None, None, None]
    w_rel = [None] * 4
    piece = rs_finish(0, cps0)
    cps1 = ag_start(0, piece.astype(BF))
    w_cps[1] = w_direct(1)
    for cp in bulk[2:]:
        cp.wait()
    x = ag_finish(0, cps1) + pos_rows
    pending = cps0 + cps1

    blk_row = lax.broadcasted_iota(jnp.int32, (8, 8 * 64), 0)
    blk_lane = lax.broadcasted_iota(jnp.int32, (8, 8 * 64), 1)
    diag = blk_row == blk_lane // 64

    def spread(qd):
        return [jnp.where(diag, jnp.concatenate([qd[8 * m:8 * m + 8]] * 4, axis=1), 0.0).astype(BF) for m in range(n_blk)]

    def attend(qd, keys, vals, masks):
        lhs = spread(qd)
        outs = []
        weights = []
        for m in range(n_blk):
            kb = keys[8 * m:8 * m + 8]
            s = dot(lhs[m], kb.reshape(8 * 64, kb.shape[-1])) * 0.125
            if masks is not None:
                s = jnp.where(masks[m], s, -1e30)
            peak = jnp.max(s, axis=-1, keepdims=True)
            e = jnp.exp(s - peak)
            weights.append((e / jnp.sum(e, axis=-1, keepdims=True)).astype(BF))
        for m in range(n_blk):
            vb = vals[8 * m:8 * m + 8]
            r = jnp.where(diag, dot_nt(weights[m], vb.reshape(8 * 64, vb.shape[-1])), 0.0)
            y = (r[:, 0:128] + r[:, 128:256]) + (r[:, 256:384] + r[:, 384:512])
            outs.append(y + pltpu.roll(y, 64, 1))
        return jnp.concatenate(outs, axis=0).astype(BF)

    t_len = kc.shape[-1]
    t_lane = lax.broadcasted_iota(jnp.int32, (8, t_len), 1)
    t_row = lax.broadcasted_iota(jnp.int32, (8, t_len), 0)
    masks = []
    for m in range(n_blk):
        lim = jnp.zeros((8, t_len), jnp.int32)
        for j in range(8):
            lim = jnp.where(t_row == j, jnp.full((8, t_len), pos[8 * m + j], jnp.int32), lim)
        masks.append(t_lane <= lim)
    lane_t = lax.broadcasted_iota(jnp.int32, (64, t_len), 1)

    for l in range(n_layers):
        s_self, s_cross = 2 * l, 2 * l + 1
        h = layer_norm(x, lns_v[l, 0, 0:1], lns_v[l, 0, 1:2])
        wq, wk, wv = wqkv_v[l, 0], wqkv_v[l, 1], wqkv_v[l, 2]
        bq, bv = inb_v[l, 0], inb_v[l, 1]
        qd = (dot_nt(h, jnp.concatenate([wq, wq], axis=0)) + jnp.concatenate([bq, bq], axis=1)).astype(BF).astype(F32)
        kv = dot_nt(h, jnp.concatenate([wk, wv], axis=0)) + jnp.concatenate([jnp.zeros_like(bv), bv], axis=1)
        kv_t = kv.astype(BF).astype(F32).T
        k_load[l].wait()
        v_load[l].wait()
        for b in range(n_seq):
            hit = lane_t == pos[b]
            kcol = jnp.broadcast_to(kv_t[0:64, b:b + 1], (64, t_len)).astype(BF)
            vcol = jnp.broadcast_to(kv_t[64:128, b:b + 1], (64, t_len)).astype(BF)
            kc[l, b] = jnp.where(hit, kcol, kc[l, b])
            vc[l, b] = jnp.where(hit, vcol, vc[l, b])
        o = attend(qd, kc.at[l], vc.at[l], masks)
        cps = o_start(s_self, o)
        pending += cps
        w_rel[s_self] = w_relay(s_self, w_cps[s_self])
        if l == 0:
            w_cps[2] = w_direct(2)
            for cp in late:
                cp.wait()
        o_full = o_finish(s_self, cps)
        w_finish(s_self, w_cps[s_self], w_rel[s_self])
        x = x + dot(o_full, wo_full[s_self].reshape(N_DEV * 64, depth)).astype(BF).astype(F32) + outb_v[0, l:l + 1]
        h = layer_norm(x, lns_v[l, 1, 0:1], lns_v[l, 1, 1:2])
        wc, bc = wcq_v[l], inb_v[l, 2]
        qd = (dot_nt(h, jnp.concatenate([wc, wc], axis=0)) + jnp.concatenate([bc, bc], axis=1)).astype(BF).astype(F32)
        ck_load[l].wait()
        cv_load[l].wait()
        o = attend(qd, cross.at[cross_slot[l][0]], cross.at[cross_slot[l][1]], None)
        cps = o_start(s_cross, o)
        pending += cps
        w_rel[s_cross] = w_relay(s_cross, w_cps[s_cross])
        if l == 0:
            cv_load[1] = local(cv.at[1], cross.at[0], cross_sem.at[3])
            w_cps[3] = w_direct(3)
        o_full = o_finish(s_cross, cps)
        w_finish(s_cross, w_cps[s_cross], w_rel[s_cross])
        x = x + dot(o_full, wo_full[s_cross].reshape(N_DEV * 64, depth)).astype(BF).astype(F32) + outb_v[1, l:l + 1]
        h = layer_norm(x, lns_v[l, 2, 0:1], lns_v[l, 2, 1:2])
        act = gelu(dot(h, wf1_v[l]) + bf1_v[l:l + 1]).astype(BF)
        cps = rs_start(1 + l, dot(act, wf2_v[l]))
        piece = rs_finish(1 + l, cps)
        cps2 = ag_start(1 + l, piece.astype(BF))
        pending += cps + cps2
        x = x + ag_finish(1 + l, cps2) + outb_v[2, l:l + 1]
    fin[...] = layer_norm(x, lnf_v[0:1], lnf_v[1:2])
    for cp in pending:
        cp.wait_send()
    for s in range(4):
        for cp in w_cps[s].values():
            cp.wait_send()
        for cp in w_rel[s].values():
            cp.wait_send()


def head_kernel(kc, vc, e_v, fin, logits, nk, nv, out_v, sem, lsem):
    n_layers = kc.shape[0]
    cps = []
    for l in range(n_layers):
        for i, (s, d) in enumerate(((kc, nk), (vc, nv))):
            cp = pltpu.make_async_copy(s.at[l], d.at[l], sem.at[i, l])
            cp.start()
            cps.append(cp)
    h = fin[...]
    rows = e_v.shape[0]
    width = 384
    for c in range(rows // width):
        out_v[:, c * width:(c + 1) * width] = dot_nt(h, e_v[c * width:(c + 1) * width])
    cp = pltpu.make_async_copy(out_v, logits, lsem)
    cp.start()
    cp.wait()
    for cp in cps:
        cp.wait()


def solution(mesh):
    any_spec = pl.BlockSpec(memory_space=pl.ANY)
    vmem = pl.BlockSpec(memory_space=pltpu.VMEM)
    smem = pl.BlockSpec(memory_space=pltpu.SMEM)

    def hbm(a):
        return pltpu.with_memory_space_constraint(a, pltpu.HBM)

    def local_step(tokens, positions, self_keys, self_vals, cross_keys, cross_vals, embed_table, pos_table, w_qkv, w_cq, in_bias, w_out, out_bias, w_fc1, b_fc1, w_fc2, ln_layers, ln_final):
        n_layers, n_seq, t_len = self_keys.shape[:3]
        frames = cross_keys.shape[2]
        depth = embed_table.shape[1]

        def cols(c):
            return jnp.transpose(c, (0, 1, 3, 4, 2)).reshape(n_layers, n_seq, 64, c.shape[2])

        args = [cols(self_keys), cols(self_vals), cols(cross_keys), cols(cross_vals), embed_table.reshape(-1, 8, depth), pos_table.reshape(-1, 8, depth),
                jnp.transpose(w_qkv, (0, 2, 3, 4, 1)).reshape(n_layers, 3, 64, depth),
                jnp.transpose(w_cq, (0, 2, 3, 1)).reshape(n_layers, 64, depth),
                in_bias, w_out.reshape(n_layers, 2, 64, depth), jnp.transpose(out_bias, (1, 0, 2)),
                w_fc1, b_fc1, w_fc2, ln_layers, ln_final]
        hidden = w_fc1.shape[2]
        dma = pltpu.SemaphoreType.DMA
        kc, vc, e_v, fin = pl.pallas_call(
            chain_kernel,
            out_shape=(pltpu.VMEM((n_layers, n_seq, 64, t_len), BF), pltpu.VMEM((n_layers, n_seq, 64, t_len), BF),
                       pltpu.VMEM((embed_table.shape[0] // 8, 8, depth), BF), pltpu.VMEM((n_seq, depth), BF)),
            in_specs=[smem, smem] + [any_spec] * len(args),
            out_specs=(vmem, vmem, vmem, vmem),
            scratch_shapes=[
                pltpu.VMEM((3, n_seq, 64, frames), BF),
                pltpu.VMEM((pos_table.shape[0] // 8, 8, depth), BF),
                pltpu.VMEM((n_layers, 3, 64, depth), BF),
                pltpu.VMEM((n_layers, 64, depth), BF),
                pltpu.VMEM(in_bias.shape, F32),
                pltpu.VMEM((3, n_layers, depth), F32),
                pltpu.VMEM((n_layers, depth, hidden), BF),
                pltpu.VMEM((n_layers, hidden), F32),
                pltpu.VMEM((n_layers, hidden, depth), BF),
                pltpu.VMEM(ln_layers.shape, F32),
                pltpu.VMEM(ln_final.shape, F32),
                pltpu.VMEM((2 * n_layers, N_DEV, 64, depth), BF),
                pltpu.VMEM((1 + n_layers, N_DEV, n_seq // 2, 128), F32),
                pltpu.VMEM((1 + n_layers, N_DEV, n_seq // 2, 128), F32),
                pltpu.VMEM((1 + n_layers, N_DEV, n_seq // 2, 128), BF),
                pltpu.VMEM((2 * n_layers, N_DEV, n_seq, 128), BF),
                dma((11,)), dma((2, n_layers)), dma((4,)), dma((2 * n_layers,)),
                dma((1 + n_layers, N_DEV)), dma((1 + n_layers, N_DEV)),
                dma((1 + n_layers, N_DEV)), dma((1 + n_layers, N_DEV)),
                dma((2 * n_layers, N_DEV)), dma((2 * n_layers, N_DEV)),
                dma((2 * n_layers, N_DEV)), dma((2 * n_layers, N_DEV)),
            ],
            compiler_params=pltpu.CompilerParams(collective_id=0, has_side_effects=True, vmem_limit_bytes=40 * 2 ** 20),
            name='chain',
        )(tokens, positions, *[hbm(a) for a in args])

        logits, nk, nv = pl.pallas_call(
            head_kernel,
            out_shape=(jax.ShapeDtypeStruct((n_seq, embed_table.shape[0]), F32),
                       jax.ShapeDtypeStruct(kc.shape, BF), jax.ShapeDtypeStruct(vc.shape, BF)),
            in_specs=[vmem] * 4,
            out_specs=(any_spec, any_spec, any_spec),
            scratch_shapes=[pltpu.VMEM((n_seq, embed_table.shape[0]), F32), dma((2, n_layers)), dma],
            compiler_params=pltpu.CompilerParams(vmem_limit_bytes=40 * 2 ** 20),
            name='head',
        )(*[pltpu.with_memory_space_constraint(a, pltpu.VMEM) for a in (kc, vc, e_v.reshape(embed_table.shape), fin)])

        def uncols(c):
            return jnp.transpose(c.reshape(n_layers, n_seq, 1, 64, t_len), (0, 1, 4, 2, 3))

        return logits, uncols(nk), uncols(nv)

    batch_spec = P('dp')
    cache_spec = P(None, 'dp', None, 'tp', None)
    in_specs = (batch_spec, batch_spec, cache_spec, cache_spec, cache_spec, cache_spec, P('tp', None), P(None, None), P(None, None, None, 'tp', None), P(None, None, 'tp', None), P(None, None, 'tp', None), P(None, None, 'tp', None, None), P(None, None, None), P(None, None, 'tp'), P(None, 'tp'), P(None, 'tp', None), P(None, None, None, None), P(None, None))
    out_specs = (P('dp', 'tp'), cache_spec, cache_spec)
    return jax.shard_map(local_step, mesh=mesh, in_specs=in_specs, out_specs=out_specs, check_vma=False)
```

time: 243 us -> 65.3 us (0.27)
  blocking collectives: 172 us -> 0 us
  Pallas kernels: 0 us -> 64.5 us
  matrix products: 42.5 us -> 0 us
  other arithmetic: 17.6 us -> 0 us
  local copies, waits for them, and re-layouts: 8.97 us -> 0 us
    psum x7 -> x0, blocking collectives: 172 us -> none  [the longest x6 146 us: group_sum(): return lax.psum(part_sum, 'tp').astype(jnp.bfloat16).astype(jnp.float32)]
    pallas_call x0 -> x2, Pallas kernels: none -> 64.5 us  [the longest x1 59.4 us: local_step(): pl.pallas_call(chain_kernel, out_shape=(pltpu.VMEM((n_layers, n_seq, 64,...]
    dot_general x19 -> x0, matrix products: 42.5 us -> none  [the longest x2 12.5 us: cross_attend(): jnp.einsum('bht,bthe->bhe', weights, val_rows, preferred_element_type=jnp...]
    select_n x3 -> x0, other arithmetic: 8.82 us -> none  [the longest x1 8.08 us: local_step(): jnp.where(write_mask, jnp.stack(new_val_rows)[:, :, None], self_vals)]
    gather x2 -> x0, local copies, waits for them, and re-layouts: 5.09 us -> none  [the longest x1 4.43 us: local_step(): jnp.take(embed_table, jnp.clip(local_ids, 0, shard_rows - 1), axis=0)]
    reduce_sum x18 -> x0, other arithmetic: 3.78 us -> none  [the longest x7 1.29 us: layer_norm(): variance = jnp.mean(centred * centred, axis=-1, keepdims=True)]
where the time goes in v1:
time: 65.3 us; the launch traced here: 65.1 us
  Pallas kernels  64.5 us (99%)
    pallas_call x1, Pallas kernels, local_step(): pl.pallas_call(chain_kernel, out_shape=(pltpu.VMEM((n_layers, n_seq, 64,...  59.4 us
    pallas_call x1, Pallas kernels, local_step(): pl.pallas_call(head_kernel, out_shape=(jax.ShapeDtypeStruct((n_seq, embed...  5.06 us

profile of v1, /device:TPU:0, one launch (start us, length us, event | category | flops | bytes accessed | tf_op | source)
XLA Modules:
  0.0 65.1 jit_solution(12552598824913319869)
XLA Ops:
  0.6 59.4 %chain.1 = (bf16[2,48,64,448]{3,2,1,0:T(8,128)(2,1)S(1)}, bf16[2,48,64,448]{3,2,1,0:T(8,128)(2,1)S(1)}, bf16[816,8,512]{2,1,0:T(8,128)(2,1)S(1)}, bf16[48,512]{1,0:T(8,128)(2,1)S(1)}) custom-call(s32[48]{0:T(128)} %tok.1, s32[48]{0:T(128)} %pos.1, bf16[2,48,64,448]{3,2,1,0:T(8,128)(2,1)} %bitcast.49, bf16[2,48,64,448]{3,2,1,0:T(8,128)(2,1)} %bitcast.50, ...), custom_call_target="tpu_custom_call" | custom-call | tf_op jit(solution)/shard_map/chain/pallas_call | solution.py:319
  60.1 5.1 %head.1 = (f32[48,6528]{1,0:T(8,128)}, bf16[2,48,64,448]{3,2,1,0:T(8,128)(2,1)}, bf16[2,48,64,448]{3,2,1,0:T(8,128)(2,1)}) custom-call(bf16[2,48,64,448]{3,2,1,0:T(8,128)(2,1)S(1)} %get-tuple-element.10.kc, bf16[2,48,64,448]{3,2,1,0:T(8,128)(2,1)S(1)} %get-tuple-element.11.vc, bf16[6528,512]{1,0:T(8,128)(2,1)S(1)} %bitcast.45, ...), custom_call_target="tpu_custom_call" | custom-call | tf_op jit(solution)/shard_map/head/pallas_call | solution.py:352

commit v2 on v1

v2 whole, which is shorter than its diff:
```python
import functools

import jax
import jax.numpy as jnp
from jax import lax
from jax.experimental import pallas as pl
from jax.experimental.pallas import tpu as pltpu
from jax.sharding import PartitionSpec as P

MESH = pl.DeviceIdType.MESH
BF = jnp.bfloat16
F32 = jnp.float32
NT = (((1,), (1,)), ((), ()))
N_DEV = 8
ROWS = 16
CHIP_PEERS = (2, 4, 6)


def dot(a, b):
    return jnp.dot(a, b, preferred_element_type=F32)


def dot_nt(a, b):
    return lax.dot_general(a, b, NT, preferred_element_type=F32)


def layer_norm(x, gain, shift):
    mean = jnp.mean(x, axis=-1, keepdims=True)
    centred = x - mean
    var = jnp.mean(centred * centred, axis=-1, keepdims=True)
    return (centred * lax.rsqrt(var + 1e-5) * gain + shift).astype(BF)


def gelu(x):
    return 0.5 * x * (1.0 + lax.erf(x * (0.5 ** 0.5)))


def chain_kernel(tok_h, pos_h, sk, sv, ck, cv, emb, ptab, wqkv, wcq, inb, wout, outb, wf1, bf1, wf2, lns, lnf,
                 kc, vc, e_v, fin,
                 tok, pos, cross, pt_v, wqkv_v, wcq_v, inb_v, outb_v, wf1_v, bf1_v, wf2_v, lns_v, lnf_v, wo_full,
                 emb_buf, rs_src, rs_dst, ag_buf, o_buf,
                 load_sem, kv_sem, cross_sem, wo_sem,
                 e_s, e_r, rs_s, rs_r, ag_s, ag_r, o_s, o_r, w_s, w_r):
    me = lax.axis_index('tp')
    n_seq, depth = fin.shape
    n_layers = kc.shape[0]
    groups = n_seq // ROWS
    g_blk = ROWS // 8
    shard_rows = e_v.shape[0] * 8
    t_len = kc.shape[-1]

    def local(src, dst, sem):
        cp = pltpu.make_async_copy(src, dst, sem)
        cp.start()
        return cp

    sends = []

    def exchange(src_of, dst_of, s_sem, r_sem, peers=tuple(range(1, N_DEV))):
        cps = {}
        for k in peers:
            cp = pltpu.make_async_remote_copy(src_ref=src_of(k), dst_ref=dst_of(k), send_sem=s_sem(k), recv_sem=r_sem(k),
                                              device_id={'tp': me ^ k}, device_id_type=MESH)
            cp.start()
            cps[k] = cp
            sends.append(cp)
        return cps

    def arrived(cps):
        for cp in cps.values():
            cp.wait_recv()

    scalars = [local(tok_h, tok, load_sem.at[0]), local(pos_h, pos, load_sem.at[1])]
    wo_own = [local(wout.at[0, 0], wo_full.at[0, me], wo_sem.at[0])]
    tables = [local(emb, e_v, load_sem.at[2]), local(ptab, pt_v, load_sem.at[3])]
    small = [(lns, lns_v), (lnf, lnf_v), (inb, inb_v), (outb, outb_v), (bf1, bf1_v), (wqkv, wqkv_v)]
    small = [local(s, d, load_sem.at[4 + i]) for i, (s, d) in enumerate(small)]
    k_load = [local(sk.at[0], kc.at[0], kv_sem.at[0, 0]), None]
    v_load = [local(sv.at[0], vc.at[0], kv_sem.at[1, 0]), None]
    wo_own += [local(wout.at[s // 2, s % 2], wo_full.at[s, me], wo_sem.at[s]) for s in range(1, 4)]
    late = [local(s, d, load_sem.at[10 + i]) for i, (s, d) in enumerate([(wcq, wcq_v), (wf1, wf1_v), (wf2, wf2_v)])]
    ck_load = [local(ck.at[0], cross.at[0], cross_sem.at[0]), None]
    cv_load = [local(cv.at[0], cross.at[1], cross_sem.at[1]), None]
    k_load[1] = local(sk.at[1], kc.at[1], kv_sem.at[0, 1])
    v_load[1] = local(sv.at[1], vc.at[1], kv_sem.at[1, 1])
    ck_load[1] = local(ck.at[1], cross.at[2], cross_sem.at[2])
    cross_slot = ((0, 1), (2, 0))

    bar = pltpu.get_barrier_semaphore()
    for k in range(1, N_DEV):
        pl.semaphore_signal(bar, inc=1, device_id={'tp': me ^ k}, device_id_type=MESH)
    pl.semaphore_wait(bar, N_DEV - 1)

    w_cps = [None] * 4
    w_rel = [None] * 4

    def w_direct(s):
        wo_own[s].wait()
        w_cps[s] = exchange(lambda k: wo_full.at[s, me], lambda k: wo_full.at[s, me],
                            lambda k: w_s.at[s, k], lambda k: w_r.at[s, k], (2, 4, 6, 1))

    def w_relay(s):
        w_rel[s] = []
        for k in CHIP_PEERS:
            w_cps[s][k].wait_recv()
            cp = pltpu.make_async_remote_copy(src_ref=wo_full.at[s, me ^ k], dst_ref=wo_full.at[s, me ^ k],
                                              send_sem=w_s.at[s, k ^ 1], recv_sem=w_r.at[s, k ^ 1],
                                              device_id={'tp': me ^ 1}, device_id_type=MESH)
            cp.start()
            w_rel[s].append(cp)
            sends.append(cp)

    def w_finish(s):
        w_cps[s][1].wait_recv()
        for cp in w_rel[s]:
            cp.wait_recv()

    w_direct(0)

    pick_row = lax.broadcasted_iota(jnp.int32, (8, 64), 0)
    pick_lane = lax.broadcasted_iota(jnp.int32, (8, 64), 1)

    def pick_rows(table, g, index_of, ok_of):
        blocks = []
        for m in range(g_blk):
            rows = []
            want = jnp.full((8, 64), -1, jnp.int32)
            for j in range(8):
                b = ROWS * g + 8 * m + j
                i = index_of(b)
                rows.append(table[lax.div(i, 8)].astype(F32))
                at = 8 * j + lax.rem(i, 8)
                if ok_of is not None:
                    at = jnp.where(ok_of(b), at, -1)
                want = jnp.where(pick_row == j, at, want)
            one_hot = jnp.where(pick_lane == want, 1.0, 0.0).astype(BF)
            blocks.append(dot(one_hot, jnp.concatenate(rows, axis=0).astype(BF)))
        return jnp.concatenate(blocks, axis=0)

    first = me * shard_rows

    def owned(b):
        loc = tok[b] - first
        return jnp.logical_and(loc >= 0, loc < shard_rows)

    for cp in scalars:
        cp.wait()
    tables[0].wait()
    emb_cps = []
    for g in range(groups):
        emb_buf[g, me] = pick_rows(e_v, g, lambda b: jnp.clip(tok[b] - first, 0, shard_rows - 1), owned).astype(BF)
        emb_cps.append(exchange(lambda k: emb_buf.at[g, me], lambda k: emb_buf.at[g, me], lambda k: e_s.at[g, k], lambda k: e_r.at[g, k]))
    tables[1].wait()
    pos_rows = [pick_rows(pt_v, g, lambda b: pos[b], None) for g in range(groups)]
    for cp in small:
        cp.wait()

    diag = lax.broadcasted_iota(jnp.int32, (8, 8 * 64), 0) == lax.broadcasted_iota(jnp.int32, (8, 8 * 64), 1) // 64
    lane128 = lax.broadcasted_iota(jnp.int32, (ROWS, 128), 1)
    t_lane = lax.broadcasted_iota(jnp.int32, (8, t_len), 1)
    t_row = lax.broadcasted_iota(jnp.int32, (8, t_len), 0)
    lane_t = lax.broadcasted_iota(jnp.int32, (64, t_len), 1)
    limits = []
    for m in range(n_seq // 8):
        lim = jnp.zeros((8, t_len), jnp.int32)
        for j in range(8):
            lim = jnp.where(t_row == j, pos[8 * m + j], lim)
        limits.append(lim)

    def scores(qd, m, keys):
        lhs = jnp.where(diag, jnp.concatenate([qd[8 * m:8 * m + 8]] * 4, axis=1), 0.0).astype(BF)
        return dot(lhs, keys.reshape(8 * 64, keys.shape[-1])) * 0.125

    def mix(w, vals):
        r = jnp.where(diag, dot_nt(w, vals.reshape(8 * 64, vals.shape[-1])), 0.0)
        y = (r[:, 0:128] + r[:, 128:256]) + (r[:, 256:384] + r[:, 384:512])
        return y + pltpu.roll(y, 64, 1)

    def o_start(s, g, o):
        o_buf[s, g, me] = o.astype(BF)
        i = s * groups + g
        return exchange(lambda k: o_buf.at[s, g, me], lambda k: o_buf.at[s, g, me], lambda k: o_s.at[i, k], lambda k: o_r.at[i, k])

    def o_finish(s, g, cps):
        arrived(cps)
        pieces = [jnp.where(lane128 < 64, o_buf[s, g, 2 * c].astype(F32), o_buf[s, g, 2 * c + 1].astype(F32)) for c in range(4)]
        o_full = jnp.concatenate(pieces, axis=1).astype(BF)
        return dot(o_full, wo_full[s].reshape(N_DEV * 64, depth)).astype(BF).astype(F32)

    half = ROWS // 2

    def rs_start(l, g, part):
        for p in range(N_DEV):
            rs_src[l, g, p] = part[half * (p % 2):half * (p % 2) + half, 128 * (p // 2):128 * (p // 2) + 128]
        i = l * groups + g
        return exchange(lambda k: rs_src.at[l, g, me ^ k], lambda k: rs_dst.at[l, g, k], lambda k: rs_s.at[i, k], lambda k: rs_r.at[i, k])

    def ag_start(l, g, cps):
        arrived(cps)
        total = rs_src[l, g, me]
        for k in range(1, N_DEV):
            total = total + rs_dst[l, g, k]
        ag_buf[l, g, me] = total.astype(BF)
        i = l * groups + g
        return exchange(lambda k: ag_buf.at[l, g, me], lambda k: ag_buf.at[l, g, me], lambda k: ag_s.at[i, k], lambda k: ag_r.at[i, k])

    def ag_finish(l, g, cps):
        arrived(cps)
        cols = [jnp.concatenate([ag_buf[l, g, 2 * c].astype(F32), ag_buf[l, g, 2 * c + 1].astype(F32)], axis=0) for c in range(4)]
        return jnp.concatenate(cols, axis=1)

    def self_stage(l, g, x):
        h = layer_norm(x, lns_v[l, 0, 0:1], lns_v[l, 0, 1:2])
        wq, wk, wv = wqkv_v[l, 0], wqkv_v[l, 1], wqkv_v[l, 2]
        bq, bv = inb_v[l, 0], inb_v[l, 1]
        qd = (dot_nt(h, jnp.concatenate([wq, wq], axis=0)) + jnp.concatenate([bq, bq], axis=1)).astype(BF).astype(F32)
        kv = dot_nt(h, jnp.concatenate([wk, wv], axis=0)) + jnp.concatenate([jnp.zeros_like(bv), bv], axis=1)
        kv = kv.astype(BF).astype(F32)
        vd = jnp.where(lane128 < 64, pltpu.roll(kv, 64, 1), kv)
        new_score = jnp.sum(jnp.where(lane128 < 64, qd * kv, 0.0), axis=-1, keepdims=True) * 0.125
        if g == 0:
            k_load[l].wait()
            v_load[l].wait()
        outs = []
        for m in range(g_blk):
            lim = limits[g * g_blk + m]
            rows = pl.ds(ROWS * g + 8 * m, 8)
            sn = new_score[8 * m:8 * m + 8]
            sc = jnp.where(t_lane < lim, scores(qd, m, kc[l, rows]), -1e30)
            peak = jnp.maximum(jnp.max(sc, axis=-1, keepdims=True), sn)
            e = jnp.exp(sc - peak)
            en = jnp.exp(sn - peak)
            den = jnp.sum(e, axis=-1, keepdims=True) + en
            w_new = (en / den).astype(BF).astype(F32)
            outs.append(mix((e / den).astype(BF), vc[l, rows]) + w_new * vd[8 * m:8 * m + 8])
        return o_start(2 * l, g, jnp.concatenate(outs, axis=0)), kv

    def patch(l, g, kv):
        kv_t = kv.T
        for j in range(ROWS):
            b = ROWS * g + j
            hit = lane_t == pos[b]
            kcol = jnp.broadcast_to(kv_t[0:64, j:j + 1], (64, t_len)).astype(BF)
            vcol = jnp.broadcast_to(kv_t[64:128, j:j + 1], (64, t_len)).astype(BF)
            kc[l, b] = jnp.where(hit, kcol, kc[l, b])
            vc[l, b] = jnp.where(hit, vcol, vc[l, b])

    def cross_stage(l, g, x, cps):
        x = x + o_finish(2 * l, g, cps) + outb_v[0, l:l + 1]
        h = layer_norm(x, lns_v[l, 1, 0:1], lns_v[l, 1, 1:2])
        wc, bc = wcq_v[l], inb_v[l, 2]
        qd = (dot_nt(h, jnp.concatenate([wc, wc], axis=0)) + jnp.concatenate([bc, bc], axis=1)).astype(BF).astype(F32)
        if g == 0:
            ck_load[l].wait()
            cv_load[l].wait()
        ks, vs = cross_slot[l]
        weights = []
        for m in range(g_blk):
            sc = scores(qd, m, cross[ks, pl.ds(ROWS * g + 8 * m, 8)])
            e = jnp.exp(sc - jnp.max(sc, axis=-1, keepdims=True))
            weights.append((e / jnp.sum(e, axis=-1, keepdims=True)).astype(BF))
        outs = [mix(weights[m], cross[vs, pl.ds(ROWS * g + 8 * m, 8)]) for m in range(g_blk)]
        return x, o_start(2 * l + 1, g, jnp.concatenate(outs, axis=0))

    def mlp_stage(l, g, x, cps):
        x = x + o_finish(2 * l + 1, g, cps) + outb_v[1, l:l + 1]
        h = layer_norm(x, lns_v[l, 2, 0:1], lns_v[l, 2, 1:2])
        act = gelu(dot(h, wf1_v[l]) + bf1_v[l:l + 1]).astype(BF)
        return x, rs_start(l, g, dot(act, wf2_v[l]))

    x = [None] * groups
    cps = emb_cps
    for l in range(n_layers):
        kvs = []
        for g in range(groups):
            if l == 0:
                arrived(cps[g])
                total = emb_buf[g, 0].astype(F32)
                for p in range(1, N_DEV):
                    total = total + emb_buf[g, p].astype(F32)
                x[g] = total + pos_rows[g]
                if g == 0:
                    w_relay(0)
            else:
                x[g] = x[g] + ag_finish(l - 1, g, cps[g]) + outb_v[2, l - 1:l]
            cps[g], kv = self_stage(l, g, x[g])
            kvs.append(kv)
        if l == 0:
            w_direct(1)
        else:
            w_relay(3)
        for g in range(groups):
            patch(l, g, kvs[g])
        w_finish(2 * l)
        if l == 0:
            for cp in late:
                cp.wait()
        for g in range(groups):
            x[g], cps[g] = cross_stage(l, g, x[g], cps[g])
            if l == 0 and g == 1:
                w_relay(1)
        if l == 0:
            cv_load[1] = local(cv.at[1], cross.at[0], cross_sem.at[3])
            w_direct(2)
        w_finish(2 * l + 1)
        for g in range(groups):
            x[g], cps[g] = mlp_stage(l, g, x[g], cps[g])
        if l == 0:
            w_relay(2)
            w_direct(3)
        cps = [ag_start(l, g, cps[g]) for g in range(groups)]
    for g in range(groups):
        x[g] = x[g] + ag_finish(n_layers - 1, g, cps[g]) + outb_v[2, n_layers - 1:n_layers]
        fin[ROWS * g:ROWS * g + ROWS] = layer_norm(x[g], lnf_v[0:1], lnf_v[1:2])
    for cp in sends:
        cp.wait_send()


def head_kernel(kc, vc, e_v, fin, logits, nk, nv, out_v, sem, lsem):
    n_layers = kc.shape[0]
    cps = []
    for l in range(n_layers):
        for i, (s, d) in enumerate(((kc, nk), (vc, nv))):
            cp = pltpu.make_async_copy(s.at[l], d.at[l], sem.at[i, l])
            cp.start()
            cps.append(cp)
    h = fin[...]
    rows = e_v.shape[0]
    width = 384
    for c in range(rows // width):
        out_v[:, c * width:(c + 1) * width] = dot_nt(h, e_v[c * width:(c + 1) * width])
    cp = pltpu.make_async_copy(out_v, logits, lsem)
    cp.start()
    cp.wait()
    for cp in cps:
        cp.wait()


def solution(mesh):
    any_spec = pl.BlockSpec(memory_space=pl.ANY)
    vmem = pl.BlockSpec(memory_space=pltpu.VMEM)

    def hbm(a):
        return pltpu.with_memory_space_constraint(a, pltpu.HBM)

    def local_step(tokens, positions, self_keys, self_vals, cross_keys, cross_vals, embed_table, pos_table, w_qkv, w_cq, in_bias, w_out, out_bias, w_fc1, b_fc1, w_fc2, ln_layers, ln_final):
        n_layers, n_seq, t_len = self_keys.shape[:3]
        frames = cross_keys.shape[2]
        depth = embed_table.shape[1]

        def cols(c):
            return jnp.transpose(c, (0, 1, 3, 4, 2)).reshape(n_layers, n_seq, 64, c.shape[2])

        args = [cols(self_keys), cols(self_vals), cols(cross_keys), cols(cross_vals), embed_table.reshape(-1, 8, depth), pos_table.reshape(-1, 8, depth),
                jnp.transpose(w_qkv, (0, 2, 3, 4, 1)).reshape(n_layers, 3, 64, depth),
                jnp.transpose(w_cq, (0, 2, 3, 1)).reshape(n_layers, 64, depth),
                in_bias, w_out.reshape(n_layers, 2, 64, depth), jnp.transpose(out_bias, (1, 0, 2)),
                w_fc1, b_fc1, w_fc2, ln_layers, ln_final]
        hidden = w_fc1.shape[2]
        groups = n_seq // ROWS
        dma = pltpu.SemaphoreType.DMA
        kc, vc, e_v, fin = pl.pallas_call(
            chain_kernel,
            out_shape=(pltpu.VMEM((n_layers, n_seq, 64, t_len), BF), pltpu.VMEM((n_layers, n_seq, 64, t_len), BF),
                       pltpu.VMEM((embed_table.shape[0] // 8, 8, depth), BF), pltpu.VMEM((n_seq, depth), BF)),
            in_specs=[any_spec] * (2 + len(args)),
            out_specs=(vmem, vmem, vmem, vmem),
            scratch_shapes=[
                pltpu.SMEM((n_seq,), jnp.int32), pltpu.SMEM((n_seq,), jnp.int32),
                pltpu.VMEM((3, n_seq, 64, frames), BF),
                pltpu.VMEM((pos_table.shape[0] // 8, 8, depth), BF),
                pltpu.VMEM((n_layers, 3, 64, depth), BF),
                pltpu.VMEM((n_layers, 64, depth), BF),
                pltpu.VMEM(in_bias.shape, F32),
                pltpu.VMEM((3, n_layers, depth), F32),
                pltpu.VMEM((n_layers, depth, hidden), BF),
                pltpu.VMEM((n_layers, hidden), F32),
                pltpu.VMEM((n_layers, hidden, depth), BF),
                pltpu.VMEM(ln_layers.shape, F32),
                pltpu.VMEM(ln_final.shape, F32),
                pltpu.VMEM((2 * n_layers, N_DEV, 64, depth), BF),
                pltpu.VMEM((groups, N_DEV, ROWS, depth), BF),
                pltpu.VMEM((n_layers, groups, N_DEV, ROWS // 2, 128), F32),
                pltpu.VMEM((n_layers, groups, N_DEV, ROWS // 2, 128), F32),
                pltpu.VMEM((n_layers, groups, N_DEV, ROWS // 2, 128), BF),
                pltpu.VMEM((2 * n_layers, groups, N_DEV, ROWS, 128), BF),
                dma((13,)), dma((2, n_layers)), dma((4,)), dma((2 * n_layers,)),
                dma((groups, N_DEV)), dma((groups, N_DEV)),
                dma((n_layers * groups, N_DEV)), dma((n_layers * groups, N_DEV)),
                dma((n_layers * groups, N_DEV)), dma((n_layers * groups, N_DEV)),
                dma((2 * n_layers * groups, N_DEV)), dma((2 * n_layers * groups, N_DEV)),
                dma((2 * n_layers, N_DEV)), dma((2 * n_layers, N_DEV)),
            ],
            compiler_params=pltpu.CompilerParams(collective_id=0, has_side_effects=True, vmem_limit_bytes=40 * 2 ** 20),
            name='chain',
        )(tokens, positions, *[hbm(a) for a in args])

        logits, nk, nv = pl.pallas_call(
            head_kernel,
            out_shape=(jax.ShapeDtypeStruct((n_seq, embed_table.shape[0]), F32),
                       jax.ShapeDtypeStruct(kc.shape, BF), jax.ShapeDtypeStruct(vc.shape, BF)),
            in_specs=[vmem] * 4,
            out_specs=(any_spec, any_spec, any_spec),
            scratch_shapes=[pltpu.VMEM((n_seq, embed_table.shape[0]), F32), dma((2, n_layers)), dma],
            compiler_params=pltpu.CompilerParams(vmem_limit_bytes=40 * 2 ** 20),
            name='head',
        )(*[pltpu.with_memory_space_constraint(a, pltpu.VMEM) for a in (kc, vc, e_v.reshape(embed_table.shape), fin)])

        def uncols(c):
            return jnp.transpose(c.reshape(n_layers, n_seq, 1, 64, t_len), (0, 1, 4, 2, 3))

        return logits, uncols(nk), uncols(nv)

    batch_spec = P('dp')
    cache_spec = P(None, 'dp', None, 'tp', None)
    in_specs = (batch_spec, batch_spec, cache_spec, cache_spec, cache_spec, cache_spec, P('tp', None), P(None, None), P(None, None, None, 'tp', None), P(None, None, 'tp', None), P(None, None, 'tp', None), P(None, None, 'tp', None, None), P(None, None, None), P(None, None, 'tp'), P(None, 'tp'), P(None, 'tp', None), P(None, None, None, None), P(None, None))
    out_specs = (P('dp', 'tp'), cache_spec, cache_spec)
    return jax.shard_map(local_step, mesh=mesh, in_specs=in_specs, out_specs=out_specs, check_vma=False)
```

time: 65.3 us -> 67.5 us (1.034)
  Pallas kernels: 64.5 us -> 66.8 us
    pallas_call x1, Pallas kernels: 59.4 us -> 61.7 us  [local_step(): pl.pallas_call(chain_kernel, out_shape=(pltpu.VMEM((n_layers, n_seq, 64,...]
where the time goes in v2:
time: 67.5 us; the launch traced here: 67.4 us
  Pallas kernels  66.8 us (99%)
    pallas_call x1, Pallas kernels, local_step(): pl.pallas_call(chain_kernel, out_shape=(pltpu.VMEM((n_layers, n_seq, 64,...  61.7 us
    pallas_call x1, Pallas kernels, local_step(): pl.pallas_call(head_kernel, out_shape=(jax.ShapeDtypeStruct((n_seq, embed...  5.06 us

profile of v2, /device:TPU:0, one launch (start us, length us, event | category | flops | bytes accessed | tf_op | source)
XLA Modules:
  0.0 67.4 jit_solution(13635804109097626344)
XLA Ops:
  0.6 61.7 %chain.1 = (bf16[2,48,64,448]{3,2,1,0:T(8,128)(2,1)S(1)}, bf16[2,48,64,448]{3,2,1,0:T(8,128)(2,1)S(1)}, bf16[816,8,512]{2,1,0:T(8,128)(2,1)S(1)}, bf16[48,512]{1,0:T(8,128)(2,1)S(1)}) custom-call(s32[48]{0:T(128)} %tok_h.1, s32[48]{0:T(128)} %pos_h.1, bf16[2,48,64,448]{3,2,1,0:T(8,128)(2,1)} %bitcast.49, bf16[2,48,64,448]{3,2,1,0:T(8,128)(2,1)} %bitcast.50, ...), custom_call_target="tpu_custom_call" | custom-call | tf_op jit(solution)/shard_map/chain/pallas_call | solution.py:362
  62.4 5.1 %head.1 = (f32[48,6528]{1,0:T(8,128)}, bf16[2,48,64,448]{3,2,1,0:T(8,128)(2,1)}, bf16[2,48,64,448]{3,2,1,0:T(8,128)(2,1)}) custom-call(bf16[2,48,64,448]{3,2,1,0:T(8,128)(2,1)S(1)} %get-tuple-element.10.kc, bf16[2,48,64,448]{3,2,1,0:T(8,128)(2,1)S(1)} %get-tuple-element.11.vc, bf16[6528,512]{1,0:T(8,128)(2,1)S(1)} %bitcast.45, ...), custom_call_target="tpu_custom_call" | custom-call | tf_op jit(solution)/shard_map/head/pallas_call | solution.py:398

commit v3 on v2

--- a/solution.py
+++ b/solution.py
@@ -54,21 +54,13 @@
         cp.start()
         return cp
 
-    sends = []
-
     def exchange(src_of, dst_of, s_sem, r_sem, peers=tuple(range(1, N_DEV))):
-        cps = {}
         for k in peers:
-            cp = pltpu.make_async_remote_copy(src_ref=src_of(k), dst_ref=dst_of(k), send_sem=s_sem(k), recv_sem=r_sem(k),
-                                              device_id={'tp': me ^ k}, device_id_type=MESH)
-            cp.start()
-            cps[k] = cp
-            sends.append(cp)
-        return cps
-
-    def arrived(cps):
-        for cp in cps.values():
-            cp.wait_recv()
+            pltpu.make_async_remote_copy(src_ref=src_of(k), dst_ref=dst_of(k), send_sem=s_sem, recv_sem=r_sem,
+                                         device_id={'tp': me ^ k}, device_id_type=MESH).start()
+
+    def arrived(buf, sem):
+        pltpu.make_async_copy(buf, buf, sem).wait()
 
     scalars = [local(tok_h, tok, load_sem.at[0]), local(pos_h, pos, load_sem.at[1])]
     wo_own = [local(wout.at[0, 0], wo_full.at[0, me], wo_sem.at[0])]
@@ -91,29 +83,18 @@
         pl.semaphore_signal(bar, inc=1, device_id={'tp': me ^ k}, device_id_type=MESH)
     pl.semaphore_wait(bar, N_DEV - 1)
 
-    w_cps = [None] * 4
-    w_rel = [None] * 4
-
     def w_direct(s):
         wo_own[s].wait()
-        w_cps[s] = exchange(lambda k: wo_full.at[s, me], lambda k: wo_full.at[s, me],
-                            lambda k: w_s.at[s, k], lambda k: w_r.at[s, k], (2, 4, 6, 1))
+        exchange(lambda k: wo_full.at[s, me], lambda k: wo_full.at[s, me], w_s, w_r.at[0, s], CHIP_PEERS)
+        exchange(lambda k: wo_full.at[s, me], lambda k: wo_full.at[s, me], w_s, w_r.at[1, s], (1,))
 
     def w_relay(s):
-        w_rel[s] = []
+        arrived(wo_full.at[s, 0:3], w_r.at[0, s])
         for k in CHIP_PEERS:
-            w_cps[s][k].wait_recv()
-            cp = pltpu.make_async_remote_copy(src_ref=wo_full.at[s, me ^ k], dst_ref=wo_full.at[s, me ^ k],
-                                              send_sem=w_s.at[s, k ^ 1], recv_sem=w_r.at[s, k ^ 1],
-                                              device_id={'tp': me ^ 1}, device_id_type=MESH)
-            cp.start()
-            w_rel[s].append(cp)
-            sends.append(cp)
+            exchange(lambda _: wo_full.at[s, me ^ k], lambda _: wo_full.at[s, me ^ k], w_s, w_r.at[1, s], (1,))
 
     def w_finish(s):
-        w_cps[s][1].wait_recv()
-        for cp in w_rel[s]:
-            cp.wait_recv()
+        arrived(wo_full.at[s, 0:4], w_r.at[1, s])
 
     w_direct(0)
 
@@ -146,10 +127,9 @@
     for cp in scalars:
         cp.wait()
     tables[0].wait()
-    emb_cps = []
     for g in range(groups):
         emb_buf[g, me] = pick_rows(e_v, g, lambda b: jnp.clip(tok[b] - first, 0, shard_rows - 1), owned).astype(BF)
-        emb_cps.append(exchange(lambda k: emb_buf.at[g, me], lambda k: emb_buf.at[g, me], lambda k: e_s.at[g, k], lambda k: e_r.at[g, k]))
+        exchange(lambda k: emb_buf.at[g, me], lambda k: emb_buf.at[g, me], e_s, e_r.at[g])
     tables[1].wait()
     pos_rows = [pick_rows(pt_v, g, lambda b: pos[b], None) for g in range(groups)]
     for cp in small:
@@ -178,11 +158,10 @@
 
     def o_start(s, g, o):
         o_buf[s, g, me] = o.astype(BF)
-        i = s * groups + g
-        return exchange(lambda k: o_buf.at[s, g, me], lambda k: o_buf.at[s, g, me], lambda k: o_s.at[i, k], lambda k: o_r.at[i, k])
-
-    def o_finish(s, g, cps):
-        arrived(cps)
+        exchange(lambda k: o_buf.at[s, g, me], lambda k: o_buf.at[s, g, me], o_s, o_r.at[s * groups + g])
+
+    def o_finish(s, g):
+        arrived(o_buf.at[s, g, 0:N_DEV - 1], o_r.at[s * groups + g])
         pieces = [jnp.where(lane128 < 64, o_buf[s, g, 2 * c].astype(F32), o_buf[s, g, 2 * c + 1].astype(F32)) for c in range(4)]
         o_full = jnp.concatenate(pieces, axis=1).astype(BF)
         return dot(o_full, wo_full[s].reshape(N_DEV * 64, depth)).astype(BF).astype(F32)
@@ -192,20 +171,18 @@
     def rs_start(l, g, part):
         for p in range(N_DEV):
             rs_src[l, g, p] = part[half * (p % 2):half * (p % 2) + half, 128 * (p // 2):128 * (p // 2) + 128]
-        i = l * groups + g
-        return exchange(lambda k: rs_src.at[l, g, me ^ k], lambda k: rs_dst.at[l, g, k], lambda k: rs_s.at[i, k], lambda k: rs_r.at[i, k])
-
-    def ag_start(l, g, cps):
-        arrived(cps)
+        exchange(lambda k: rs_src.at[l, g, me ^ k], lambda k: rs_dst.at[l, g, k], rs_s, rs_r.at[l * groups + g])
+
+    def ag_start(l, g):
+        arrived(rs_dst.at[l, g, 1:N_DEV], rs_r.at[l * groups + g])
         total = rs_src[l, g, me]
         for k in range(1, N_DEV):
             total = total + rs_dst[l, g, k]
         ag_buf[l, g, me] = total.astype(BF)
-        i = l * groups + g
-        return exchange(lambda k: ag_buf.at[l, g, me], lambda k: ag_buf.at[l, g, me], lambda k: ag_s.at[i, k], lambda k: ag_r.at[i, k])
-
-    def ag_finish(l, g, cps):
-        arrived(cps)
+        exchange(lambda k: ag_buf.at[l, g, me], lambda k: ag_buf.at[l, g, me], ag_s, ag_r.at[l * groups + g])
+
+    def ag_finish(l, g):
+        arrived(ag_buf.at[l, g, 0:N_DEV - 1], ag_r.at[l * groups + g])
         cols = [jnp.concatenate([ag_buf[l, g, 2 * c].astype(F32), ag_buf[l, g, 2 * c + 1].astype(F32)], axis=0) for c in range(4)]
         return jnp.concatenate(cols, axis=1)
 
@@ -233,7 +210,8 @@
             den = jnp.sum(e, axis=-1, keepdims=True) + en
             w_new = (en / den).astype(BF).astype(F32)
             outs.append(mix((e / den).astype(BF), vc[l, rows]) + w_new * vd[8 * m:8 * m + 8])
-        return o_start(2 * l, g, jnp.concatenate(outs, axis=0)), kv
+        o_start(2 * l, g, jnp.concatenate(outs, axis=0))
+        return kv
 
     def patch(l, g, kv):
         kv_t = kv.T
@@ -245,8 +223,8 @@
             kc[l, b] = jnp.where(hit, kcol, kc[l, b])
             vc[l, b] = jnp.where(hit, vcol, vc[l, b])
 
-    def cross_stage(l, g, x, cps):
-        x = x + o_finish(2 * l, g, cps) + outb_v[0, l:l + 1]
+    def cross_stage(l, g, x):
+        x = x + o_finish(2 * l, g) + outb_v[0, l:l + 1]
         h = layer_norm(x, lns_v[l, 1, 0:1], lns_v[l, 1, 1:2])
         wc, bc = wcq_v[l], inb_v[l, 2]
         qd = (dot_nt(h, jnp.concatenate([wc, wc], axis=0)) + jnp.concatenate([bc, bc], axis=1)).astype(BF).astype(F32)
@@ -260,21 +238,22 @@
             e = jnp.exp(sc - jnp.max(sc, axis=-1, keepdims=True))
             weights.append((e / jnp.sum(e, axis=-1, keepdims=True)).astype(BF))
         outs = [mix(weights[m], cross[vs, pl.ds(ROWS * g + 8 * m, 8)]) for m in range(g_blk)]
-        return x, o_start(2 * l + 1, g, jnp.concatenate(outs, axis=0))
-
-    def mlp_stage(l, g, x, cps):
-        x = x + o_finish(2 * l + 1, g, cps) + outb_v[1, l:l + 1]
+        o_start(2 * l + 1, g, jnp.concatenate(outs, axis=0))
+        return x
+
+    def mlp_stage(l, g, x):
+        x = x + o_finish(2 * l + 1, g) + outb_v[1, l:l + 1]
         h = layer_norm(x, lns_v[l, 2, 0:1], lns_v[l, 2, 1:2])
         act = gelu(dot(h, wf1_v[l]) + bf1_v[l:l + 1]).astype(BF)
-        return x, rs_start(l, g, dot(act, wf2_v[l]))
+        rs_start(l, g, dot(act, wf2_v[l]))
+        return x
 
     x = [None] * groups
-    cps = emb_cps
     for l in range(n_layers):
         kvs = []
         for g in range(groups):
             if l == 0:
-                arrived(cps[g])
+                arrived(emb_buf.at[g, 0:N_DEV - 1], e_r.at[g])
                 total = emb_buf[g, 0].astype(F32)
                 for p in range(1, N_DEV):
                     total = total + emb_buf[g, p].astype(F32)
@@ -282,9 +261,8 @@
                 if g == 0:
                     w_relay(0)
             else:
-                x[g] = x[g] + ag_finish(l - 1, g, cps[g]) + outb_v[2, l - 1:l]
-            cps[g], kv = self_stage(l, g, x[g])
-            kvs.append(kv)
+                x[g] = x[g] + ag_finish(l - 1, g) + outb_v[2, l - 1:l]
+            kvs.append(self_stage(l, g, x[g]))
         if l == 0:
             w_direct(1)
         else:
@@ -296,7 +274,7 @@
             for cp in late:
                 cp.wait()
         for g in range(groups):
-            x[g], cps[g] = cross_stage(l, g, x[g], cps[g])
+            x[g] = cross_stage(l, g, x[g])
             if l == 0 and g == 1:
                 w_relay(1)
         if l == 0:
@@ -304,16 +282,20 @@
             w_direct(2)
         w_finish(2 * l + 1)
         for g in range(groups):
-            x[g], cps[g] = mlp_stage(l, g, x[g], cps[g])
+            x[g] = mlp_stage(l, g, x[g])
         if l == 0:
             w_relay(2)
             w_direct(3)
-        cps = [ag_start(l, g, cps[g]) for g in range(groups)]
+        for g in range(groups):
+            ag_start(l, g)
     for g in range(groups):
-        x[g] = x[g] + ag_finish(n_layers - 1, g, cps[g]) + outb_v[2, n_layers - 1:n_layers]
+        x[g] = x[g] + ag_finish(n_layers - 1, g) + outb_v[2, n_layers - 1:n_layers]
         fin[ROWS * g:ROWS * g + ROWS] = layer_norm(x[g], lnf_v[0:1], lnf_v[1:2])
-    for cp in sends:
-        cp.wait_send()
+    arrived(emb_buf.at[:, 0:N_DEV - 1], e_s)
+    arrived(o_buf.at[:, :, 0:N_DEV - 1], o_s)
+    arrived(rs_src.at[:, :, 0:N_DEV - 1], rs_s)
+    arrived(ag_buf.at[:, :, 0:N_DEV - 1], ag_s)
+    arrived(wo_full.at[:, 0:N_DEV - 1], w_s)
 
 
 def head_kernel(kc, vc, e_v, fin, logits, nk, nv, out_v, sem, lsem):
@@ -385,11 +367,8 @@
                 pltpu.VMEM((n_layers, groups, N_DEV, ROWS // 2, 128), BF),
                 pltpu.VMEM((2 * n_layers, groups, N_DEV, ROWS, 128), BF),
                 dma((13,)), dma((2, n_layers)), dma((4,)), dma((2 * n_layers,)),
-                dma((groups, N_DEV)), dma((groups, N_DEV)),
-                dma((n_layers * groups, N_DEV)), dma((n_layers * groups, N_DEV)),
-                dma((n_layers * groups, N_DEV)), dma((n_layers * groups, N_DEV)),
-                dma((2 * n_layers * groups, N_DEV)), dma((2 * n_layers * groups, N_DEV)),
-                dma((2 * n_layers, N_DEV)), dma((2 * n_layers, N_DEV)),
+                dma, dma((groups,)), dma, dma((n_layers * groups,)), dma, dma((n_layers * groups,)),
+                dma, dma((2 * n_layers * groups,)), dma, dma((2, 2 * n_layers)),
             ],
             compiler_params=pltpu.CompilerParams(collective_id=0, has_side_effects=True, vmem_limit_bytes=40 * 2 ** 20),
             name='chain',

time: 67.5 us -> 63 us (0.933)
  Pallas kernels: 66.8 us -> 62.3 us
    pallas_call x1, Pallas kernels: 61.7 us -> 57.2 us  [local_step(): pl.pallas_call(chain_kernel, out_shape=(pltpu.VMEM((n_layers, n_seq, 64,...]
where the time goes in v3:
time: 63 us; the launch traced here: 62.9 us
  Pallas kernels  62.3 us (99%)
  between operations  0.65 us (1%)
    pallas_call x1, Pallas kernels, local_step(): pl.pallas_call(chain_kernel, out_shape=(pltpu.VMEM((n_layers, n_seq, 64,...  57.2 us
    pallas_call x1, Pallas kernels, local_step(): pl.pallas_call(head_kernel, out_shape=(jax.ShapeDtypeStruct((n_seq, embed...  5.06 us

profile of v3, /device:TPU:0, one launch (start us, length us, event | category | flops | bytes accessed | tf_op | source)
XLA Modules:
  0.0 62.9 jit_solution(6623787991097101870)
XLA Ops:
  0.6 57.2 %chain.1 = (bf16[2,48,64,448]{3,2,1,0:T(8,128)(2,1)S(1)}, bf16[2,48,64,448]{3,2,1,0:T(8,128)(2,1)S(1)}, bf16[816,8,512]{2,1,0:T(8,128)(2,1)S(1)}, bf16[48,512]{1,0:T(8,128)(2,1)S(1)}) custom-call(s32[48]{0:T(128)} %tok_h.1, s32[48]{0:T(128)} %pos_h.1, bf16[2,48,64,448]{3,2,1,0:T(8,128)(2,1)} %bitcast.49, bf16[2,48,64,448]{3,2,1,0:T(8,128)(2,1)} %bitcast.50, ...), custom_call_target="tpu_custom_call" | custom-call | tf_op jit(solution)/shard_map/chain/pallas_call | solution.py:344
  57.9 5.1 %head.1 = (f32[48,6528]{1,0:T(8,128)}, bf16[2,48,64,448]{3,2,1,0:T(8,128)(2,1)}, bf16[2,48,64,448]{3,2,1,0:T(8,128)(2,1)}) custom-call(bf16[2,48,64,448]{3,2,1,0:T(8,128)(2,1)S(1)} %get-tuple-element.10.kc, bf16[2,48,64,448]{3,2,1,0:T(8,128)(2,1)S(1)} %get-tuple-element.11.vc, bf16[6528,512]{1,0:T(8,128)(2,1)S(1)} %bitcast.45, ...), custom_call_target="tpu_custom_call" | custom-call | tf_op jit(solution)/shard_map/head/pallas_call | solution.py:377
